TPU v7x, 32 devices: a whole 2x2x4 slice. The times are simulated.
32 devices in a mesh: atoms: 8 (over y, x, core), gsplit: 4 (over z).
Axes of the slice: x: 2, y: 2, z: 4, core: 2. Of those that a mesh axis runs over, the one named last changes fastest.
Arguments:
- miller: int32 [3, 30720], P(None, 'gsplit'), may hold values from -16 to 16, as said below
- form_factors: bfloat16 [49, 30720], P(None, 'gsplit'), may hold values from -6 to 6
- fractional: float32 [3, 512], P(None, 'atoms'), may hold values from 0 to 1
- multipoles: bfloat16 [2, 49, 512], P(None, None, 'atoms'), may hold values from -0.0390625 to 0.0390625
- point_owner: int32 [1024], P(('atoms', 'gsplit')), may hold values from 0 to 63
- offsets: float32 [3, 1024], P(None, ('atoms', 'gsplit')), may hold values from -0.05 to 0.05
Outputs:
- grid_potential: float32 [2, 1024], P(None, ('atoms', 'gsplit'))
- moments: float32 [2, 49, 512], P(None, None, ('atoms', 'gsplit'))
Inputs may be any that keep to these rules, and one draw needn't show every extreme that they name: `miller`: no vector has all three indices zero. Point p belongs to atom (p // 128) * 64 + point_owner[p].
All inputs are finite; a program needn't handle non-finite values.
Results may differ from a plain program's by a relative error of at most 0.0045.
Values may be sent and summed in bfloat16 or wider, within the bound.
A program may use at most 64 MiB of HBM per device.

v0:
```python
import math

import jax
import jax.numpy as jnp
from jax import lax
from jax.sharding import PartitionSpec as P

two_pi = 2.0 * math.pi
damping = 1.0 / 400.0


def angles(vectors, places):
    indices = vectors.astype(jnp.float32)
    summed = (
        places[0][:, None] * indices[0][None, :]
        + places[1][:, None] * indices[1][None, :]
        + places[2][:, None] * indices[2][None, :]
    )
    return two_pi * summed


def sign_tables(comp_count):
    comp_ids = jnp.arange(comp_count, dtype=jnp.int32)
    degree = jnp.zeros((comp_count,), jnp.int32)
    for degree_step in range(1, 16):
        degree = degree + (comp_ids >= degree_step * degree_step).astype(jnp.int32)
    quarter = degree % 4
    even_sign = jnp.where(quarter == 0, 1.0, jnp.where(quarter == 2, -1.0, 0.0)).astype(jnp.float32)
    odd_sign = jnp.where(quarter == 3, 1.0, jnp.where(quarter == 1, -1.0, 0.0)).astype(jnp.float32)
    return (even_sign, odd_sign)


def coulomb(vectors):
    indices = vectors.astype(jnp.float32)
    square = indices[0] * indices[0] + indices[1] * indices[1] + indices[2] * indices[2]
    return jnp.exp(-damping * square) / square


def structure(multipoles, cos_table, sin_table, form_block, even_sign, odd_sign):
    density_count, comp_count, atom_count = multipoles.shape
    flattened = multipoles.reshape(density_count * comp_count, atom_count)
    along_cos = jnp.dot(flattened, cos_table, preferred_element_type=jnp.float32).reshape(
        density_count, comp_count, -1
    )
    along_sin = jnp.dot(flattened, sin_table, preferred_element_type=jnp.float32).reshape(
        density_count, comp_count, -1
    )
    weights = form_block.astype(jnp.float32)[None]
    even_wide = even_sign[None, :, None]
    odd_wide = odd_sign[None, :, None]
    real_part = jnp.sum(weights * (even_wide * along_cos + odd_wide * along_sin), axis=1)
    imag_part = jnp.sum(weights * (odd_wide * along_cos - even_wide * along_sin), axis=1)
    return jnp.stack([real_part, imag_part], axis=1)


def moment_terms(potential, form_block, cos_table, sin_table, even_sign, odd_sign):
    weighted = (form_block.astype(jnp.float32)[None, None] * potential[:, :, None, :]).astype(
        jnp.bfloat16
    )
    density_count, _, comp_count, vector_count = weighted.shape
    even_rows = (even_sign != 0.0)[None, :, None]
    against_cos = jnp.where(even_rows, weighted[:, 0], weighted[:, 1]).reshape(
        density_count * comp_count, vector_count
    )
    against_sin = jnp.where(even_rows, weighted[:, 1], weighted[:, 0]).reshape(
        density_count * comp_count, vector_count
    )
    contract = (((1,), (1,)), ((), ()))
    with_cos = lax.dot_general(
        against_cos, cos_table, contract, preferred_element_type=jnp.float32
    ).reshape(density_count, comp_count, -1)
    with_sin = lax.dot_general(
        against_sin, sin_table, contract, preferred_element_type=jnp.float32
    ).reshape(density_count, comp_count, -1)
    even_wide = even_sign[None, :, None]
    odd_wide = odd_sign[None, :, None]
    return even_wide * (with_cos - with_sin) + odd_wide * (with_cos + with_sin)


def grid_rows(rounded, vectors, places):
    point_angles = angles(vectors, places)
    cos_points = jnp.cos(point_angles).astype(jnp.bfloat16)
    sin_points = jnp.sin(point_angles).astype(jnp.bfloat16)
    contract = (((1,), (1,)), ((), ()))
    return lax.dot_general(
        cos_points, rounded[:, 0], contract, preferred_element_type=jnp.float32
    ) - lax.dot_general(sin_points, rounded[:, 1], contract, preferred_element_type=jnp.float32)


def grid_blocked(rounded, vectors, places):
    point_count = places.shape[1]
    return grid_rows(rounded, vectors, places)


def shards(miller, form_factors, fractional, multipoles, point_owner, offsets):
    even_sign, odd_sign = sign_tables(form_factors.shape[0])
    phases = angles(miller, fractional)
    cos_table = jnp.cos(phases).astype(jnp.bfloat16)
    sin_table = jnp.sin(phases).astype(jnp.bfloat16)
    partial_sums = structure(multipoles, cos_table, sin_table, form_factors, even_sign, odd_sign)
    summed = lax.psum(partial_sums, "atoms")
    potential = coulomb(miller)[None, None, :] * summed
    local_moments = moment_terms(potential, form_factors, cos_table, sin_table, even_sign, odd_sign)
    moments = lax.psum_scatter(local_moments, "gsplit", scatter_dimension=2, tiled=True)
    atom_ids = jnp.arange(fractional.shape[1], dtype=jnp.int32)
    onehot = (atom_ids[:, None] == point_owner[None, :]).astype(jnp.float32)
    places = (
        jnp.dot(
            fractional, onehot, precision=lax.Precision.HIGHEST, preferred_element_type=jnp.float32
        )
        + offsets
    )
    rounded = potential.astype(jnp.bfloat16)
    every_vector = lax.all_gather(miller, "gsplit", axis=1, tiled=True)
    every_potential = lax.all_gather(rounded, "gsplit", axis=2, tiled=True)
    point_rows = grid_blocked(every_potential, every_vector, places)
    return (point_rows.T, moments)


def solution(mesh):
    placed = (
        P(None, "gsplit"),
        P(None, "gsplit"),
        P(None, "atoms"),
        P(None, None, "atoms"),
        P(("atoms", "gsplit")),
        P(None, ("atoms", "gsplit")),
    )
    return jax.shard_map(
        shards,
        mesh=mesh,
        in_specs=placed,
        out_specs=(P(None, ("atoms", "gsplit")), P(None, None, ("atoms", "gsplit"))),
        check_vma=False,
    )
```

profile of v0, /device:TPU:0, one launch (start us, length us, event | category | flops | bytes accessed | tf_op | source)
XLA Modules:
  0.0 180.9 jit_solution(15231726801209480579)
XLA Ops:
  7.2 0.0 all-reduce.3.cloned.1.call-start
  7.2 0.9 convert_element_type.435
  8.1 0.2 slice_reduce_fusion.2
  8.4 0.8 slice_bitcast_fusion.15
  9.2 0.8 copy.11
  10.0 0.1 reshape.154
  10.1 8.7 %convolution_bitcast_fusion.1 = f32[98,7680]{1,0:T(8,128)} fusion(bf16[98,64]{0,1:T(8,128)(2,1)S(1)} %reshape.154, f32[7680]{0:T(1024)S(1)} %get-tuple-element.11, f32[64]{0:T(128)S(1)} %get-tuple-element.20, f32[7680]{0:T(1024)S(1)} %get-tuple-element.12, f32[64]{0:T(128)S(1)} %get-tuple-element.19, f32[7680]{0:T(1024)S(1)} %get-tuple-element.10, ...), kind=kOutput, calls=%fused_computation.1 | convolution fusion | flops 99778560 | bytes 3116032 | tf_op jit(solution)/shard_map/dot_general | solution.py:42
  18.8 7.0 %convolution_bitcast_fusion = f32[98,7680]{1,0:T(8,128)S(1)} fusion(bf16[98,64]{0,1:T(8,128)(2,1)S(1)} %reshape.154, f32[7680]{0:T(1024)S(1)} %get-tuple-element.11, f32[64]{0:T(128)S(1)} %get-tuple-element.20, f32[7680]{0:T(1024)S(1)} %get-tuple-element.12, f32[64]{0:T(128)S(1)} %get-tuple-element.19, f32[7680]{0:T(1024)S(1)} %get-tuple-element.10, ...), kind=kOutput, calls=%fused_computation | convolution fusion | flops 99778560 | bytes 3116032 | tf_op jit(solution)/shard_map/dot_general | solution.py:45
  25.9 4.0 %reshape.155 = f32[2,49,7680]{2,1,0:T(8,128)} reshape(f32[98,7680]{1,0:T(8,128)} %convolution_bitcast_fusion.1) | data formatting | bytes 6021120 | tf_op jit(solution)/shard_map/reshape | solution.py:42
  29.8 2.1 %reshape.156 = f32[2,49,7680]{2,1,0:T(8,128)} reshape(f32[98,7680]{1,0:T(8,128)S(1)} %convolution_bitcast_fusion) | data formatting | bytes 6021120 | tf_op jit(solution)/shard_map/reshape | solution.py:45
  31.9 1.3 convert_element_type.436
  33.2 0.0 copy-start
  33.2 4.5 %multiply_reduce_fusion.1 = (f32[2,7680]{1,0:T(2,128)S(1)}, f32[2,7680]{1,0:T(2,128)S(1)}) fusion(f32[2,49,7680]{2,1,0:T(8,128)} %reshape.156, f32[2,49,7680]{2,1,0:T(8,128)} %reshape.155, f32[49]{0:T(128)S(1)} %get-tuple-element.24, f32[49]{0:T(128)S(1)} %get-tuple-element.25, f32[49,7680]{1,0:T(8,128)S(1)} %convert_element_type.436), kind=kLoop, calls=%fused_computation.7 | loop fusion | flops 7495680 | bytes 7649672 | tf_op jit(solution)/shard_map/reduce_sum | solution.py:51
  37.7 0.0 copy-start.1
  37.8 0.0 copy-start.2
  37.8 0.0 copy-start.3
  37.8 0.0 copy-start.4
  37.8 0.7 pad_maximum_fusion
  38.5 0.0 all-reduce.3.cloned.1.call-update
  38.5 0.0 copy-done
  38.6 17.6 %all_gather.7 = s32[3,30720]{1,0:T(4,128)S(1)} all-gather(s32[3,7680]{1,0:T(4,128)S(1)} %copy-done), channel_id=1, replica_groups=mesh['atoms'=8,'gsplit'=4] {'gsplit'}, dimensions={1}, use_global_device_ids=true | all-gather | bytes 460800 | tf_op jit(solution)/shard_map/all_gather | solution.py:114
  56.1 0.1 convert_element_type.455
  56.2 0.3 fusion.54
  56.5 0.0 copy-done.1
  56.5 0.0 copy-done.2
  56.5 0.0 copy-done.3
  56.5 0.1 fusion.8
  56.6 0.0 copy-done.4
  56.7 0.6 dynamic-slice
  57.9 36.2 %all-reduce.3.cloned.1.call-done = f32[2,2,7680]{2,0,1:T(2,128)} async-done(((f32[2,2,7680]{2,0,1:T(2,128)}), f32[2,2,7680]{2,0,1:T(2,128)}) %all-reduce.3.cloned.1.call-update) | async-done | bytes 122896 | tf_op jit(solution)/shard_map/psum | solution.py:101
  94.1 1.0 fusion.53
  95.1 0.4 multiply_convert_fusion
  95.5 7.4 %fusion.2 = f32[2,49,64]{2,1,0:T(8,128)S(1)} fusion(pred[49]{0:T(512)(128)(4,1)S(1)} %broadcast_compare_fusion, bf16[2,2,49,7680]{3,2,0,1:T(8,128)(2,1)S(1)} %multiply_convert_fusion, f32[7680]{0:T(1024)S(1)} %get-tuple-element.11, f32[64]{0:T(128)S(1)} %get-tuple-element.20, f32[7680]{0:T(1024)S(1)} %get-tuple-element.12, f32[64]{0:T(128)S(1)} %get-tuple-element.19, ...), kind=kOutput, calls=%fused_computation.15 | convolution fusion | flops 100531200 | bytes 3128625 | tf_op jit(solution)/shard_map/dot_general | solution.py:72
  102.9 7.5 %multiply_add_fusion = f32[2,49,64]{2,1,0:T(8,128)S(1)} fusion(f32[2,49,64]{2,1,0:T(8,128)S(1)} %fusion.2, f32[7680]{0:T(1024)S(1)} %get-tuple-element.11, f32[64]{0:T(128)S(1)} %get-tuple-element.20, f32[7680]{0:T(1024)S(1)} %get-tuple-element.12, f32[64]{0:T(128)S(1)} %get-tuple-element.19, f32[7680]{0:T(1024)S(1)} %get-tuple-element.10, ...), kind=kOutput, calls=%fused_computation.30 | convolution fusion | flops 100562560 | bytes 3154105 | tf_op jit(solution)/shard_map/dot_general | solution.py:69
  110.5 0.1 copy.12
  110.6 19.9 %all-reduce = f32[2,49,64]{1,0,2:T(2,128)S(1)} all-reduce(f32[2,49,64]{1,0,2:T(2,128)S(1)} %copy.12), channel_id=2, replica_groups=mesh['atoms'=8,'gsplit'=4] {'gsplit'}, use_global_device_ids=true, to_apply=%region_3.4.clone | all-reduce | flops 6272 | bytes 50176
  130.5 0.6 copy.13
  131.1 14.1 %all_gather.6 = bf16[2,2,30720]{2,0,1:T(2,128)(2,1)S(1)} all-gather(bf16[2,2,7680]{2,0,1:T(2,128)(2,1)S(1)} %get-tuple-element.13), channel_id=1, replica_groups=mesh['atoms'=8,'gsplit'=4] {'gsplit'}, dimensions={2}, use_global_device_ids=true | all-gather | bytes 307200 | tf_op jit(solution)/shard_map/all_gather | solution.py:115
  145.1 13.8 %fusion = f32[2,32]{1,0:T(2,128)S(1)} fusion(f32[30720]{0:T(1024)S(1)} %bitcast.69, f32[32]{0:T(128)S(1)} %get-tuple-element.22, f32[30720]{0:T(1024)S(1)} %bitcast.71, f32[32]{0:T(128)S(1)} %get-tuple-element.23, f32[30720]{0:T(1024)S(1)} %bitcast.67, f32[32]{0:T(128)S(1)} %get-tuple-element.21, bf16[2,2,30720]{2,0,1:T(2,128)(2,1)S(1)} %all_gather.6), kind=kOutput, calls=%fused_computation.11 | convolution fusion | flops 10813440 | bytes 493312 | tf_op jit(solution)/shard_map/dot_general | solution.py:85
  159.0 14.6 %fusion.9 = f32[2,32]{1,0:T(2,128)} fusion(f32[2,32]{1,0:T(2,128)S(1)} %fusion, f32[30720]{0:T(1024)S(1)} %bitcast.70, f32[32]{0:T(128)S(1)} %get-tuple-element.22, f32[30720]{0:T(1024)S(1)} %bitcast.72, f32[32]{0:T(128)S(1)} %get-tuple-element.23, f32[30720]{0:T(1024)S(1)} %bitcast.68, f32[32]{0:T(128)S(1)} %get-tuple-element.21, ...), kind=kOutput, calls=%fused_computation.23 | convolution fusion | flops 10813504 | bytes 494336 | tf_op jit(solution)/shard_map/dot_general | solution.py:87
  (5 shorter events, 0.1 us)
Async XLA Ops:
  7.2 87.0 %all-reduce.3.cloned.1.call-start = ((), (), s32[]{:S(2)}) async-start(), calls=%async_computation | async-start | bytes 245760 | tf_op jit(solution)/shard_map/psum | solution.py:101
  33.2 5.4 %copy-start = (s32[3,7680]{1,0:T(4,128)S(1)}, s32[3,7680]{1,0:T(4,128)}, u32[]{:S(2)}) copy-start(s32[3,7680]{1,0:T(4,128)} %param.6) | copy-start | bytes 276484
  37.7 18.7 %copy-start.1 = (f32[3,64]{1,0:T(4,128)S(1)}, f32[3,64]{1,0:T(4,128)}, u32[]{:S(2)}) copy-start(f32[3,64]{1,0:T(4,128)} %param.8) | copy-start | bytes 2308
  37.8 18.7 %copy-start.2 = (f32[3,32]{1,0:T(4,128)S(1)}, f32[3,32]{1,0:T(4,128)}, u32[]{:S(2)}) copy-start(f32[3,32]{1,0:T(4,128)} %param.11) | copy-start | bytes 1156
  37.8 18.7 %copy-start.3 = (s32[32]{0:T(128)S(1)}, s32[32]{0:T(128)}, u32[]{:S(2)}) copy-start(s32[32]{0:T(128)} %param.10) | copy-start | bytes 388
  37.8 18.9 %copy-start.4 = (u32[32]{0:T(128)S(1)}, u32[32]{0:T(128)}, u32[]{:S(2)}) copy-start(u32[32]{0:T(128)} %constant.62) | copy-start | bytes 388
Sparse Core Ops, SparseCore 0:
  38.6 55.4 all-reduce.2
where the time goes:
time: 184 us; the launch traced here: 181 us
  matrix products  59.2 us (32%)
  blocking collectives  51.5 us (28%)
  waiting for transfers between devices  36.2 us (20%)
  between operations  15.3 us (8%)
  local copies, waits for them, and re-layouts  9.62 us (5%)
  other arithmetic  8.97 us (5%)
    psum x1, waiting for transfers between devices, shards(): summed = lax.psum(partial_sums, 'atoms')  36.2 us
    unnamed x1, blocking collectives  19.9 us
    all_gather x1, blocking collectives, shards(): every_vector = lax.all_gather(miller, 'gsplit', axis=1, tiled=True)  17.6 us
    dot_general x1, matrix products, grid_rows(): lax.dot_general(sin_points, rounded[:, 1], contract, preferred_element_ty...  14.6 us
    all_gather x1, blocking collectives, shards(): every_potential = lax.all_gather(rounded, 'gsplit', axis=2, tiled=True)  14.1 us
    dot_general x1, matrix products, grid_rows(): lax.dot_general(cos_points, rounded[:, 0], contract, preferred_element_ty...  13.8 us
    dot_general x1, matrix products, structure(): jnp.dot(flattened, cos_table, preferred_element_type=jnp.float32)  8.67 us
    dot_general x1, matrix products, moment_terms(): lax.dot_general(against_cos, cos_table, contract, preferred_element_type=...  7.51 us
  transfers between devices with their start and end apart: 1, of which 1 were waited for; matrix products, arithmetic and copies ran while one was open for 1% of the time, Pallas kernels for 0%

commit v1 on v0

v1 whole, which is shorter than its diff:
```python
import functools

import jax
import jax.numpy as jnp
from jax import lax
from jax.experimental import pallas as pl
from jax.experimental.pallas import tpu as pltpu
from jax.sharding import PartitionSpec as P

damping = 1.0 / 400.0
MESH = pl.DeviceIdType.MESH
f32 = jnp.float32
bf16 = jnp.bfloat16

SIN_COEFS = (4.442879567546084, -7.30781668449178, 3.5977741780871235, -0.7911993921609659)
COS_COEFS = (
    1.4142134962552286,
    -6.978850948563789,
    5.73946037690675,
    -1.8835579059841712,
    0.3106880275217573,
)


def poly(coefs, x):
    total = coefs[-1]
    for coef in coefs[-2::-1]:
        total = total * x + coef
    return total


def cos_sin(turns):
    r = turns - jnp.round(turns)
    square = r * r
    half_sin = r * poly(SIN_COEFS, square)
    half_cos = poly(COS_COEFS, square)
    return (1.0 - half_sin * half_sin).astype(bf16), (half_sin * half_cos).astype(bf16)


def three_parts(x):
    first = x.astype(bf16).astype(f32)
    rest = x - first
    second = rest.astype(bf16).astype(f32)
    third = rest - second
    return jnp.concatenate([first, second, third, jnp.zeros_like(x)], axis=0)


def row_signs(comps, rows):
    ids = lax.broadcasted_iota(jnp.int32, (rows, 1), 0)
    degree = jnp.zeros_like(ids)
    for step in range(1, 16):
        if step * step < comps:
            degree = degree + (ids >= step * step).astype(jnp.int32)
    quarter = lax.rem(degree, 4)
    quarter = jnp.where(ids == comps, 0, quarter)
    even = (quarter == 0) | (quarter == 2)
    sign = jnp.where((quarter == 0) | (quarter == 3), 1.0, -1.0).astype(f32)
    return even, sign


def kernel(
    n_atoms, n_split, chunk,
    miller_ref, form_ref, frac_ref, mult_ref, owner_ref, offs_ref,
    grid_out, mom_out,
    vec8, fx, tcos, tsin, partial, from_core, acc, hop_in, total, place_buf, send_buf, recv_buf,
    core_sems, hop_send, hop_recv, back_sems, place_send, place_recv, out_send, out_recv,
):
    me = lax.axis_index("atoms")
    mine = lax.axis_index("gsplit")
    dens, comps, atoms = mult_ref.shape
    rows = fx.shape[0]
    width = partial.shape[3]
    steps = width // chunk
    points = n_split * owner_ref.shape[0]
    own_points = owner_ref.shape[0]
    bits = n_atoms.bit_length() - 1
    core = lax.rem(me, 2)
    other = 1 - core

    def flipped(bit):
        return me + (1 - 2 * lax.rem(lax.div(me, 2**bit), 2)) * 2**bit

    barrier = pltpu.get_barrier_semaphore()
    for bit in range(bits):
        pl.semaphore_signal(barrier, inc=1, device_id={"atoms": flipped(bit)}, device_id_type=MESH)
    for away in range(1, n_split):
        pl.semaphore_signal(
            barrier, inc=1, device_id={"gsplit": lax.rem(mine + away, n_split)}, device_id_type=MESH
        )

    even, sign = row_signs(comps, rows)

    vec8[...] = jnp.zeros_like(vec8)
    vec8[0:3, :] = miller_ref[...].astype(f32)

    tail = (comps // 8) * 8
    tail_ids = lax.broadcasted_iota(jnp.int32, (rows - tail, fx.shape[1]), 0)
    fx[tail:rows, :] = jnp.where(tail_ids == comps - tail, 1.0, 0.0).astype(f32)
    fx[0:comps, :] = form_ref[...].astype(f32) * sign[0:comps]

    frac8 = jnp.concatenate([frac_ref[...], jnp.zeros((5, atoms), f32)], axis=0)
    frac_parts = three_parts(frac8)
    atom_ids = lax.broadcasted_iota(jnp.int32, (atoms, own_points), 0)
    onehot = (atom_ids == owner_ref[...].reshape(1, own_points)).astype(f32).astype(bf16)
    picked = jnp.dot(frac_parts.astype(bf16), onehot, preferred_element_type=f32)
    place = (picked[0:8] + picked[8:16]) + picked[16:24]
    place_buf[mine, :, :] = jnp.zeros(place_buf.shape[1:], f32)
    place_buf[mine, :, 0:own_points] = place
    place_buf[mine, 0:3, 0:own_points] = place[0:3] + offs_ref[...]

    def widened(block):
        pad = jnp.zeros((block.shape[0], 128 - block.shape[1]), f32)
        return jnp.concatenate([block, pad], axis=1).T if pad.shape[1] else block.T

    atom_parts = widened(frac_parts)[0:atoms].astype(bf16)

    groups = []
    for part in range(2):
        for d in range(dens):
            m = jnp.concatenate(
                [mult_ref[d].astype(f32), jnp.zeros((rows - comps, atoms), f32)], axis=0
            )
            if part == 0:
                with_cos, with_sin = jnp.where(even, m, 0.0), jnp.where(even, 0.0, m)
            else:
                with_cos, with_sin = jnp.where(even, 0.0, m), jnp.where(even, -m, 0.0)
            groups.append(jnp.concatenate([with_cos, with_sin], axis=1))
    against = jnp.concatenate(groups, axis=0).astype(bf16)

    def vectors(half, quarter, i):
        start = pl.multiple_of(half * 2 * width + quarter * width + i * chunk, 128)
        return pl.ds(start, chunk)

    def turns(parts, where):
        v = vec8[:, where]
        wide = jnp.concatenate([v, v, v, jnp.zeros_like(v)], axis=0).astype(bf16)
        return jnp.dot(parts, wide, preferred_element_type=f32)

    def within(quarter, i):
        return pl.ds(pl.multiple_of(quarter * width + i * chunk, 128), chunk)

    def structure(half, quarter):
        def body(i, carry):
            where = vectors(half, quarter, i)
            inside = within(quarter, i)
            c, s = cos_sin(turns(atom_parts, where))
            tcos[half, 0:atoms, inside] = c
            tsin[half, 0:atoms, inside] = s
            both = jnp.concatenate([c, s], axis=0)
            along = jnp.dot(against, both, preferred_element_type=f32)
            f = fx[:, where]
            sums = [
                jnp.sum(f * along[k * rows : (k + 1) * rows], axis=0, keepdims=True)
                for k in range(2 * dens)
            ]
            lanes = pl.ds(pl.multiple_of(i * chunk, 128), chunk)
            partial[half, quarter, :, lanes] = jnp.concatenate(sums, axis=0)
            return carry

        lax.fori_loop(0, steps, body, 0)

    structure(other, 0)
    structure(other, 1)

    pl.semaphore_wait(barrier, bits + n_split - 1)

    place_copies = []
    for away in range(1, n_split):
        copy = pltpu.make_async_remote_copy(
            src_ref=place_buf.at[mine],
            dst_ref=place_buf.at[mine],
            send_sem=place_send.at[away],
            recv_sem=place_recv.at[away],
            device_id={"gsplit": lax.rem(mine + away, n_split)},
            device_id_type=MESH,
        )
        copy.start()
        place_copies.append(copy)
    to_core = pltpu.make_async_remote_copy(
        src_ref=partial.at[other],
        dst_ref=from_core,
        send_sem=core_sems.at[0],
        recv_sem=core_sems.at[1],
        device_id={"atoms": flipped(0)},
        device_id_type=MESH,
    )
    to_core.start()

    structure(core, 0)
    structure(core, 1)

    def hop(stage, quarter):
        bit = 1 + stage if quarter == 0 else bits - 1 - stage
        return pltpu.make_async_remote_copy(
            src_ref=acc.at[stage, quarter],
            dst_ref=hop_in.at[stage, quarter],
            send_sem=hop_send.at[stage, quarter],
            recv_sem=hop_recv.at[stage, quarter],
            device_id={"atoms": flipped(bit)},
            device_id_type=MESH,
        )

    to_core.wait()
    hops = {}
    for quarter in range(2):
        acc[0, quarter] = partial[core, quarter] + from_core[quarter]
        if bits > 1:
            hops[0, quarter] = hop(0, quarter)
            hops[0, quarter].start()

    for copy in place_copies:
        copy.wait()
    pieces = [three_parts(place_buf[k, :, 0:own_points]) for k in range(n_split)]
    point_parts = widened(jnp.concatenate(pieces, axis=1))[0:points].astype(bf16)

    def point_tables(half, quarter):
        def body(i, carry):
            inside = within(quarter, i)
            c, s = cos_sin(turns(point_parts, vectors(half, quarter, i)))
            tcos[half, atoms : atoms + points, inside] = c
            tsin[half, atoms : atoms + points, inside] = s
            return carry

        lax.fori_loop(0, steps, body, 0)

    work = [(h, q) for h in range(2) for q in range(2)]
    stages = bits - 1
    for stage in range(stages):
        share = work[stage * len(work) // stages : (stage + 1) * len(work) // stages]
        for half, quarter in share:
            point_tables(half, quarter)
        for quarter in range(2):
            hops[stage, quarter].wait()
            summed = acc[stage, quarter] + hop_in[stage, quarter]
            if stage + 1 < stages:
                acc[stage + 1, quarter] = summed
                hops[stage + 1, quarter] = hop(stage + 1, quarter)
                hops[stage + 1, quarter].start()
            else:
                total[core, quarter] = summed
    back = pltpu.make_async_remote_copy(
        src_ref=total.at[core],
        dst_ref=total.at[core],
        send_sem=back_sems.at[0],
        recv_sem=back_sems.at[1],
        device_id={"atoms": flipped(0)},
        device_id_type=MESH,
    )
    back.start()

    def moments(half):
        result = None
        for quarter in range(2):
            start = pl.multiple_of(half * 2 * width + quarter * width, 128)
            where = pl.ds(start, width)
            v = vec8[:, where]
            q = jnp.sum(v * v, axis=0, keepdims=True)
            pot = (jnp.exp(-damping * q) / q) * total[half, quarter]
            f = fx[:, where]
            lanes = slice(quarter * width, (quarter + 1) * width)
            with_cos, with_sin = [], []
            for d in range(dens):
                re, im = pot[d : d + 1], pot[dens + d : dens + d + 1]
                with_cos.append(f * jnp.where(even, re, im))
                with_sin.append(f * jnp.where(even, -im, re))
            for table, weights in ((tcos, with_cos), (tsin, with_sin)):
                term = lax.dot_general(
                    table[half, :, lanes],
                    jnp.concatenate(weights, axis=0).astype(bf16),
                    (((1,), (1,)), ((), ())),
                    preferred_element_type=f32,
                )
                result = term if result is None else result + term
        return result

    own = moments(core)
    back.wait()
    local = own + moments(other)

    pad = jnp.zeros((local.shape[0], 128 - local.shape[1]), f32)
    local = jnp.concatenate([local, pad], axis=1)
    grid_rows = local[atoms : atoms + points].T
    share = atoms // n_split
    for k in range(n_split):
        send_buf[k, 0:share, :] = local[k * share : (k + 1) * share]
        send_buf[k, share:, :] = jnp.zeros((8, 128), f32)
        for d in range(dens):
            row = d * rows + comps
            send_buf[k, share + d : share + d + 1, 0:own_points] = grid_rows[
                row : row + 1, k * own_points : (k + 1) * own_points
            ]
    out_copies = []
    for away in range(1, n_split):
        there = lax.rem(mine + away, n_split)
        copy = pltpu.make_async_remote_copy(
            src_ref=send_buf.at[there],
            dst_ref=recv_buf.at[away],
            send_sem=out_send.at[away],
            recv_sem=out_recv.at[away],
            device_id={"gsplit": there},
            device_id_type=MESH,
        )
        copy.start()
        out_copies.append(copy)
    result = send_buf[mine]
    for away, copy in enumerate(out_copies, 1):
        copy.wait()
        result = result + recv_buf[away]
    grid_out[...] = result[share : share + dens, 0:own_points]
    if share < 128:
        square = jnp.concatenate([result[0:share], jnp.zeros((128 - share, 128), f32)], axis=0)
    by_comp = square.T
    for d in range(dens):
        mom_out[d] = by_comp[d * rows : d * rows + comps, 0:share]


def shards(n_atoms, n_split, miller, form_factors, fractional, multipoles, point_owner, offsets):
    dens, comps, atoms = multipoles.shape
    vectors = miller.shape[1]
    width = vectors // 4
    chunk = max(c for c in (128, 256, 384) if width % c == 0)
    rows = (comps + 1 + 7) // 8 * 8
    own_points = point_owner.shape[0]
    table_rows = atoms + n_split * own_points
    stages = max(n_atoms.bit_length() - 2, 1)
    share = atoms // n_split
    vmem = pl.BlockSpec(memory_space=pltpu.VMEM)
    dma = pltpu.SemaphoreType.DMA
    return pl.pallas_call(
        functools.partial(kernel, n_atoms, n_split, chunk),
        out_shape=(
            jax.ShapeDtypeStruct((dens, own_points), f32),
            jax.ShapeDtypeStruct((dens, comps, share), f32),
        ),
        in_specs=[vmem] * 6,
        out_specs=(vmem, vmem),
        scratch_shapes=[
            pltpu.VMEM((8, vectors), f32),
            pltpu.VMEM((rows, vectors), f32),
            pltpu.VMEM((2, table_rows, 2 * width), bf16),
            pltpu.VMEM((2, table_rows, 2 * width), bf16),
            pltpu.VMEM((2, 2, 2 * dens, width), f32),
            pltpu.VMEM((2, 2 * dens, width), f32),
            pltpu.VMEM((stages, 2, 2 * dens, width), f32),
            pltpu.VMEM((stages, 2, 2 * dens, width), f32),
            pltpu.VMEM((2, 2, 2 * dens, width), f32),
            pltpu.VMEM((n_split, 8, 128), f32),
            pltpu.VMEM((n_split, share + 8, 128), f32),
            pltpu.VMEM((n_split, share + 8, 128), f32),
            dma((2,)),
            dma((stages, 2)),
            dma((stages, 2)),
            dma((2,)),
            dma((n_split,)),
            dma((n_split,)),
            dma((n_split,)),
            dma((n_split,)),
        ],
        compiler_params=pltpu.CompilerParams(
            collective_id=0, has_side_effects=True, vmem_limit_bytes=48 * 1024 * 1024
        ),
        name="hartree",
    )(miller, form_factors, fractional, multipoles, point_owner, offsets)


def solution(mesh):
    placed = (
        P(None, "gsplit"),
        P(None, "gsplit"),
        P(None, "atoms"),
        P(None, None, "atoms"),
        P(("atoms", "gsplit")),
        P(None, ("atoms", "gsplit")),
    )
    return jax.shard_map(
        functools.partial(shards, mesh.shape["atoms"], mesh.shape["gsplit"]),
        mesh=mesh,
        in_specs=placed,
        out_specs=(P(None, ("atoms", "gsplit")), P(None, None, ("atoms", "gsplit"))),
        check_vma=False,
    )
```

time: 184 us -> 29.2 us (0.16); the launches traced: 181 us -> 28.9 us
  matrix products: 59.2 us -> 0 us
  blocking collectives: 51.5 us -> 0 us
  waiting for transfers between devices: 36.2 us -> 0 us
  Pallas kernels: 0 us -> 24.2 us
  between operations: 15.3 us -> 0.68 us
  other arithmetic: 8.97 us -> 0 us
  local copies, waits for them, and re-layouts: 9.62 us -> 4.07 us
    dot_general x7 -> x0, matrix products: 59.2 us -> none  [the longest x1 14.6 us: grid_rows(): lax.dot_general(sin_points, rounded[:, 1], contract, preferred_element_ty...]
    psum x1 -> x0, waiting for transfers between devices: 36.2 us -> none  [shards(): summed = lax.psum(partial_sums, 'atoms')]
    all_gather x2 -> x0, blocking collectives: 31.6 us -> none  [the longest x1 17.6 us: shards(): every_vector = lax.all_gather(miller, 'gsplit', axis=1, tiled=True)]
    pallas_call x0 -> x1, Pallas kernels: none -> 24.2 us  [shards(): pl.pallas_call(functools.partial(kernel, n_atoms, n_split, chunk), out_sh...]
    unnamed x1 -> x0, blocking collectives: 19.9 us -> none
    reshape x3 -> x0, local copies, waits for them, and re-layouts: 6.13 us -> none  [the longest x1 3.95 us: structure(): jnp.dot(flattened, cos_table, preferred_element_type=jnp.float32)]
    reduce_sum x1 -> x0, other arithmetic: 4.53 us -> none  [structure(): jnp.sum(weights * (even_wide * along_cos + odd_wide * along_sin), axis=1)]
    convert_element_type x5 -> x0, other arithmetic: 3.67 us -> none  [the longest x1 1.27 us: structure(): weights = form_block.astype(jnp.float32)[None]]
  transfers between devices with their start and end apart: 1 -> 0, of which waited for: 1 -> 0; matrix products, arithmetic and copies ran while one was open for 1% -> 0% of each run, Pallas kernels for 0% -> 0%
where the time goes in v1:
time: 29.2 us; the launch traced here: 28.9 us
  Pallas kernels  24.2 us (83%)
  local copies, waits for them, and re-layouts  4.07 us (14%)
  between operations  0.68 us (2%)
    pallas_call x1, Pallas kernels, shards(): pl.pallas_call(functools.partial(kernel, n_atoms, n_split, chunk), out_sh...  24.2 us
    unnamed x12, local copies, waits for them, and re-layouts  3.39 us
    pallas_call x1, local copies, waits for them, and re-layouts, shards(): pl.pallas_call(functools.partial(kernel, n_atoms, n_split, chunk), out_sh...  0.68 us

profile of v1, /device:TPU:0, one launch (start us, length us, event | category | flops | bytes accessed | tf_op | source)
XLA Modules:
  0.0 28.9 jit_solution(8286144200505812269)
XLA Ops:
  0.6 0.0 copy-start.3
  0.6 0.0 copy-start.4
  0.7 0.0 copy-start.2
  0.7 0.8 %copy.8.mult_ref = bf16[2,49,64]{2,1,0:T(8,128)(2,1)S(1)} copy(bf16[2,49,64]{2,0,1:T(2,128)(2,1)} %param.9) | data formatting | bytes 25088 | tf_op args[3]
  1.4 0.0 copy-done.3
  1.4 0.0 copy-done.4
  1.4 0.0 copy-done.2
  1.4 0.0 copy-start
  1.5 1.1 %copy-done = bf16[49,7680]{1,0:T(8,128)(2,1)S(1)} copy-done((bf16[49,7680]{1,0:T(8,128)(2,1)S(1)}, bf16[49,7680]{1,0:T(8,128)(2,1)}, u32[]{:S(2)}) %copy-start) | copy-done | bytes 752664
  2.6 0.0 copy-start.1
  2.6 0.9 %copy-done.1 = s32[3,7680]{1,0:T(4,128)S(1)} copy-done((s32[3,7680]{1,0:T(4,128)S(1)}, s32[3,7680]{1,0:T(4,128)}, u32[]{:S(2)}) %copy-start.1) | copy-done | bytes 92184
  3.5 24.2 %hartree.1 = (f32[2,32]{1,0:T(2,128)S(1)}, f32[2,49,16]{2,1,0:T(8,128)S(1)}) custom-call(s32[3,7680]{1,0:T(4,128)S(1)} %copy-done.1, bf16[49,7680]{1,0:T(8,128)(2,1)S(1)} %copy-done, f32[3,64]{1,0:T(4,128)S(1)} %copy-done.2, bf16[2,49,64]{2,1,0:T(8,128)(2,1)S(1)} %copy.8.mult_ref, s32[32]{0:T(128)S(1)} %copy-done.4, f32[3,32]{1,0:T(4,128)S(1)} %copy-done.3), custom_call_target="tpu_custom_call" | custom-call | tf_op jit(solution)/shard_map/hartree/pallas_call | solution.py:329
  27.7 0.7 %copy.9 = f32[2,49,16]{1,2,0:T(8,128)} copy(f32[2,49,16]{2,1,0:T(8,128)S(1)} %get-tuple-element.3) | data formatting | bytes 12544 | tf_op jit(solution)/shard_map/hartree/pallas_call | solution.py:329
  28.4 0.6 %copy.11 = f32[2,32]{1,0:T(2,128)} copy(f32[2,32]{1,0:T(2,128)S(1)} %get-tuple-element.6) | data formatting | bytes 512
Async XLA Ops:
  0.6 0.8 %copy-start.3 = (f32[3,32]{1,0:T(4,128)S(1)}, f32[3,32]{1,0:T(4,128)}, u32[]{:S(2)}) copy-start(f32[3,32]{1,0:T(4,128)} %offs_ref.1) | copy-start | bytes 1156
  0.6 0.8 %copy-start.4 = (s32[32]{0:T(128)S(1)}, s32[32]{0:T(128)}, u32[]{:S(2)}) copy-start(s32[32]{0:T(128)} %owner_ref.1) | copy-start | bytes 388
  0.7 0.8 %copy-start.2 = (f32[3,64]{1,0:T(4,128)S(1)}, f32[3,64]{1,0:T(4,128)}, u32[]{:S(2)}) copy-start(f32[3,64]{1,0:T(4,128)} %frac_ref.1) | copy-start | bytes 2308
  1.4 1.2 %copy-start = (bf16[49,7680]{1,0:T(8,128)(2,1)S(1)}, bf16[49,7680]{1,0:T(8,128)(2,1)}, u32[]{:S(2)}) copy-start(bf16[49,7680]{1,0:T(8,128)(2,1)} %form_ref.1) | copy-start | bytes 2257924
  2.6 0.9 %copy-start.1 = (s32[3,7680]{1,0:T(4,128)S(1)}, s32[3,7680]{1,0:T(4,128)}, u32[]{:S(2)}) copy-start(s32[3,7680]{1,0:T(4,128)} %miller_ref.1) | copy-start | bytes 276484

commit v2 on v1

--- a/solution.py
+++ b/solution.py
@@ -60,29 +60,47 @@
 
 def kernel(
     n_atoms, n_split, chunk,
+    miller_hbm, form_hbm, frac_hbm, mult_hbm, owner_hbm, offs_hbm,
+    grid_out, mom_out,
     miller_ref, form_ref, frac_ref, mult_ref, owner_ref, offs_ref,
-    grid_out, mom_out,
-    vec8, fx, tcos, tsin, partial, from_core, acc, hop_in, total, place_buf, send_buf, recv_buf,
-    core_sems, hop_send, hop_recv, back_sems, place_send, place_recv, out_send, out_recv,
+    vec8, fx, tcos, tsin, partial, from_core, acc, chip_out, chip_in, total,
+    place_buf, send_buf, recv_buf,
+    load_sems, core_send, core_recv, chip_send, chip_recv, back_send, back_recv,
+    place_send, place_recv, out_send, out_recv,
 ):
     me = lax.axis_index("atoms")
     mine = lax.axis_index("gsplit")
-    dens, comps, atoms = mult_ref.shape
+    loads = [
+        pltpu.make_async_copy(src, dst, load_sems.at[k])
+        for k, (src, dst) in enumerate((
+            (owner_hbm, owner_ref), (offs_hbm, offs_ref), (frac_hbm, frac_ref),
+            (mult_hbm, mult_ref), (miller_hbm, miller_ref), (form_hbm, form_ref),
+        ))
+    ]
+    for load in loads:
+        load.start()
+    comps, dens, atoms = mult_ref.shape
     rows = fx.shape[0]
     width = partial.shape[3]
     steps = width // chunk
     points = n_split * owner_ref.shape[0]
     own_points = owner_ref.shape[0]
-    bits = n_atoms.bit_length() - 1
+    chips = n_atoms // 2
     core = lax.rem(me, 2)
     other = 1 - core
 
-    def flipped(bit):
-        return me + (1 - 2 * lax.rem(lax.div(me, 2**bit), 2)) * 2**bit
+    def flipped(mask):
+        there = me
+        for bit in range(mask.bit_length()):
+            if mask >> bit & 1:
+                there = there + (1 - 2 * lax.rem(lax.div(me, 2**bit), 2)) * 2**bit
+        return there
+
+    greeted = [1] + [2 * away for away in range(1, chips)]
 
     barrier = pltpu.get_barrier_semaphore()
-    for bit in range(bits):
-        pl.semaphore_signal(barrier, inc=1, device_id={"atoms": flipped(bit)}, device_id_type=MESH)
+    for mask in greeted:
+        pl.semaphore_signal(barrier, inc=1, device_id={"atoms": flipped(mask)}, device_id_type=MESH)
     for away in range(1, n_split):
         pl.semaphore_signal(
             barrier, inc=1, device_id={"gsplit": lax.rem(mine + away, n_split)}, device_id_type=MESH
@@ -90,13 +108,12 @@
 
     even, sign = row_signs(comps, rows)
 
-    vec8[...] = jnp.zeros_like(vec8)
-    vec8[0:3, :] = miller_ref[...].astype(f32)
-
     tail = (comps // 8) * 8
     tail_ids = lax.broadcasted_iota(jnp.int32, (rows - tail, fx.shape[1]), 0)
     fx[tail:rows, :] = jnp.where(tail_ids == comps - tail, 1.0, 0.0).astype(f32)
-    fx[0:comps, :] = form_ref[...].astype(f32) * sign[0:comps]
+    vec8[...] = jnp.zeros_like(vec8)
+    for load in loads[:4]:
+        load.wait()
 
     frac8 = jnp.concatenate([frac_ref[...], jnp.zeros((5, atoms), f32)], axis=0)
     frac_parts = three_parts(frac8)
@@ -114,11 +131,12 @@
 
     atom_parts = widened(frac_parts)[0:atoms].astype(bf16)
 
+    multipoles = mult_ref[...].astype(f32)
     groups = []
     for part in range(2):
         for d in range(dens):
             m = jnp.concatenate(
-                [mult_ref[d].astype(f32), jnp.zeros((rows - comps, atoms), f32)], axis=0
+                [multipoles[:, d, :], jnp.zeros((rows - comps, atoms), f32)], axis=0
             )
             if part == 0:
                 with_cos, with_sin = jnp.where(even, m, 0.0), jnp.where(even, 0.0, m)
@@ -148,6 +166,7 @@
             tsin[half, 0:atoms, inside] = s
             both = jnp.concatenate([c, s], axis=0)
             along = jnp.dot(against, both, preferred_element_type=f32)
+            fx[0:comps, where] = form_ref[:, where].astype(f32) * sign[0:comps]
             f = fx[:, where]
             sums = [
                 jnp.sum(f * along[k * rows : (k + 1) * rows], axis=0, keepdims=True)
@@ -157,12 +176,15 @@
             partial[half, quarter, :, lanes] = jnp.concatenate(sums, axis=0)
             return carry
 
-        lax.fori_loop(0, steps, body, 0)
+        lax.fori_loop(0, steps, body, 0, unroll=steps)
+
+    loads[4].wait()
+    vec8[0:3, :] = miller_ref[...].astype(f32)
+    loads[5].wait()
 
     structure(other, 0)
-    structure(other, 1)
-
-    pl.semaphore_wait(barrier, bits + n_split - 1)
+
+    pl.semaphore_wait(barrier, len(greeted) + n_split - 1)
 
     place_copies = []
     for away in range(1, n_split):
@@ -176,37 +198,62 @@
         )
         copy.start()
         place_copies.append(copy)
-    to_core = pltpu.make_async_remote_copy(
-        src_ref=partial.at[other],
-        dst_ref=from_core,
-        send_sem=core_sems.at[0],
-        recv_sem=core_sems.at[1],
-        device_id={"atoms": flipped(0)},
-        device_id_type=MESH,
-    )
-    to_core.start()
-
-    structure(core, 0)
-    structure(core, 1)
-
-    def hop(stage, quarter):
-        bit = 1 + stage if quarter == 0 else bits - 1 - stage
-        return pltpu.make_async_remote_copy(
-            src_ref=acc.at[stage, quarter],
-            dst_ref=hop_in.at[stage, quarter],
-            send_sem=hop_send.at[stage, quarter],
-            recv_sem=hop_recv.at[stage, quarter],
-            device_id={"atoms": flipped(bit)},
+
+    def to_core(quarter):
+        copy = pltpu.make_async_remote_copy(
+            src_ref=partial.at[other, quarter],
+            dst_ref=from_core.at[quarter],
+            send_sem=core_send.at[quarter],
+            recv_sem=core_recv.at[quarter],
+            device_id={"atoms": flipped(1)},
             device_id_type=MESH,
         )
-
-    to_core.wait()
-    hops = {}
-    for quarter in range(2):
-        acc[0, quarter] = partial[core, quarter] + from_core[quarter]
-        if bits > 1:
-            hops[0, quarter] = hop(0, quarter)
-            hops[0, quarter].start()
+        copy.start()
+        return copy
+
+    def to_chips(quarter, arriving):
+        arriving.wait()
+        summed = partial[core, quarter] + from_core[quarter]
+        acc[quarter] = summed
+        chip_out[quarter] = summed.astype(bf16)
+        copies = []
+        for away in range(1, chips):
+            copy = pltpu.make_async_remote_copy(
+                src_ref=chip_out.at[quarter],
+                dst_ref=chip_in.at[away, quarter],
+                send_sem=chip_send.at[away, quarter],
+                recv_sem=chip_recv.at[away, quarter],
+                device_id={"atoms": flipped(2 * away)},
+                device_id_type=MESH,
+            )
+            copy.start()
+            copies.append(copy)
+        return copies
+
+    def back(quarter, copies):
+        summed = acc[quarter]
+        for away, copy in enumerate(copies, 1):
+            copy.wait()
+            summed = summed + chip_in[away, quarter].astype(f32)
+        total[core, quarter] = summed
+        copy = pltpu.make_async_remote_copy(
+            src_ref=total.at[core, quarter],
+            dst_ref=total.at[core, quarter],
+            send_sem=back_send.at[quarter],
+            recv_sem=back_recv.at[quarter],
+            device_id={"atoms": flipped(1)},
+            device_id_type=MESH,
+        )
+        copy.start()
+        return copy
+
+    first = to_core(0)
+    structure(core, 0)
+    structure(other, 1)
+    second = to_core(1)
+    first = to_chips(0, first)
+    structure(core, 1)
+    second = to_chips(1, second)
 
     for copy in place_copies:
         copy.wait()
@@ -223,30 +270,12 @@
 
         lax.fori_loop(0, steps, body, 0)
 
-    work = [(h, q) for h in range(2) for q in range(2)]
-    stages = bits - 1
-    for stage in range(stages):
-        share = work[stage * len(work) // stages : (stage + 1) * len(work) // stages]
-        for half, quarter in share:
-            point_tables(half, quarter)
-        for quarter in range(2):
-            hops[stage, quarter].wait()
-            summed = acc[stage, quarter] + hop_in[stage, quarter]
-            if stage + 1 < stages:
-                acc[stage + 1, quarter] = summed
-                hops[stage + 1, quarter] = hop(stage + 1, quarter)
-                hops[stage + 1, quarter].start()
-            else:
-                total[core, quarter] = summed
-    back = pltpu.make_async_remote_copy(
-        src_ref=total.at[core],
-        dst_ref=total.at[core],
-        send_sem=back_sems.at[0],
-        recv_sem=back_sems.at[1],
-        device_id={"atoms": flipped(0)},
-        device_id_type=MESH,
-    )
-    back.start()
+    point_tables(0, 0)
+    point_tables(0, 1)
+    first = back(0, first)
+    point_tables(1, 0)
+    point_tables(1, 1)
+    second = back(1, second)
 
     def moments(half):
         result = None
@@ -274,7 +303,8 @@
         return result
 
     own = moments(core)
-    back.wait()
+    first.wait()
+    second.wait()
     local = own + moments(other)
 
     pad = jnp.zeros((local.shape[0], 128 - local.shape[1]), f32)
@@ -293,8 +323,8 @@
     for away in range(1, n_split):
         there = lax.rem(mine + away, n_split)
         copy = pltpu.make_async_remote_copy(
-            src_ref=send_buf.at[there],
-            dst_ref=recv_buf.at[away],
+            src_ref=send_buf.at[there, 0 : share + dens],
+            dst_ref=recv_buf.at[away, 0 : share + dens],
             send_sem=out_send.at[away],
             recv_sem=out_recv.at[away],
             device_id={"gsplit": there},
@@ -302,16 +332,13 @@
         )
         copy.start()
         out_copies.append(copy)
-    result = send_buf[mine]
+    result = send_buf[mine, 0 : share + dens]
     for away, copy in enumerate(out_copies, 1):
         copy.wait()
-        result = result + recv_buf[away]
+        result = result + recv_buf[away, 0 : share + dens]
     grid_out[...] = result[share : share + dens, 0:own_points]
-    if share < 128:
-        square = jnp.concatenate([result[0:share], jnp.zeros((128 - share, 128), f32)], axis=0)
-    by_comp = square.T
     for d in range(dens):
-        mom_out[d] = by_comp[d * rows : d * rows + comps, 0:share]
+        mom_out[d] = result[0:share, d * rows : d * rows + comps]
 
 
 def shards(n_atoms, n_split, miller, form_factors, fractional, multipoles, point_owner, offsets):
@@ -322,34 +349,45 @@
     rows = (comps + 1 + 7) // 8 * 8
     own_points = point_owner.shape[0]
     table_rows = atoms + n_split * own_points
-    stages = max(n_atoms.bit_length() - 2, 1)
+    chips = n_atoms // 2
     share = atoms // n_split
     vmem = pl.BlockSpec(memory_space=pltpu.VMEM)
     dma = pltpu.SemaphoreType.DMA
-    return pl.pallas_call(
+    hbm = pl.BlockSpec(memory_space=pltpu.HBM)
+    grid, moments = pl.pallas_call(
         functools.partial(kernel, n_atoms, n_split, chunk),
         out_shape=(
             jax.ShapeDtypeStruct((dens, own_points), f32),
-            jax.ShapeDtypeStruct((dens, comps, share), f32),
+            jax.ShapeDtypeStruct((dens, share, comps), f32),
         ),
-        in_specs=[vmem] * 6,
+        in_specs=[hbm] * 6,
         out_specs=(vmem, vmem),
         scratch_shapes=[
+            pltpu.VMEM(miller.shape, miller.dtype),
+            pltpu.VMEM(form_factors.shape, form_factors.dtype),
+            pltpu.VMEM(fractional.shape, fractional.dtype),
+            pltpu.VMEM((comps, dens, atoms), multipoles.dtype),
+            pltpu.VMEM(point_owner.shape, point_owner.dtype),
+            pltpu.VMEM(offsets.shape, offsets.dtype),
             pltpu.VMEM((8, vectors), f32),
             pltpu.VMEM((rows, vectors), f32),
             pltpu.VMEM((2, table_rows, 2 * width), bf16),
             pltpu.VMEM((2, table_rows, 2 * width), bf16),
             pltpu.VMEM((2, 2, 2 * dens, width), f32),
             pltpu.VMEM((2, 2 * dens, width), f32),
-            pltpu.VMEM((stages, 2, 2 * dens, width), f32),
-            pltpu.VMEM((stages, 2, 2 * dens, width), f32),
+            pltpu.VMEM((2, 2 * dens, width), f32),
+            pltpu.VMEM((2, 2 * dens, width), bf16),
+            pltpu.VMEM((chips, 2, 2 * dens, width), bf16),
             pltpu.VMEM((2, 2, 2 * dens, width), f32),
             pltpu.VMEM((n_split, 8, 128), f32),
             pltpu.VMEM((n_split, share + 8, 128), f32),
             pltpu.VMEM((n_split, share + 8, 128), f32),
+            dma((6,)),
             dma((2,)),
-            dma((stages, 2)),
-            dma((stages, 2)),
+            dma((2,)),
+            dma((chips, 2)),
+            dma((chips, 2)),
+            dma((2,)),
             dma((2,)),
             dma((n_split,)),
             dma((n_split,)),
@@ -357,10 +395,18 @@
             dma((n_split,)),
         ],
         compiler_params=pltpu.CompilerParams(
-            collective_id=0, has_side_effects=True, vmem_limit_bytes=48 * 1024 * 1024
+            collective_id=0, has_side_effects=True, vmem_limit_bytes=67_043_328
         ),
         name="hartree",
-    )(miller, form_factors, fractional, multipoles, point_owner, offsets)
+    )(
+        miller,
+        form_factors,
+        fractional,
+        jnp.transpose(multipoles, (1, 0, 2)),
+        point_owner,
+        offsets,
+    )
+    return grid, jnp.transpose(moments, (0, 2, 1))
 
 
 def solution(mesh):

time: 29.2 us -> 25.9 us (0.89)
  Pallas kernels: 24.2 us -> 22.4 us
  local copies, waits for them, and re-layouts: 4.07 us -> 2.54 us
    pallas_call x1, Pallas kernels: 24.2 us -> 22.4 us  [shards(): pl.pallas_call(functools.partial(kernel, n_atoms, n_split, chunk), out_sh...]
    unnamed x12 -> x4, local copies, waits for them, and re-layouts: 3.39 us -> 2.54 us
    pallas_call x1 -> x0, local copies, waits for them, and re-layouts: 0.68 us -> none  [shards(): pl.pallas_call(functools.partial(kernel, n_atoms, n_split, chunk), out_sh...]
where the time goes in v2:
time: 25.9 us; the launch traced here: 25.6 us
  Pallas kernels  22.4 us (86%)
  local copies, waits for them, and re-layouts  2.54 us (10%)
  between operations  0.65 us (3%)
    pallas_call x1, Pallas kernels, shards(): pl.pallas_call(functools.partial(kernel, n_atoms, n_split, chunk), out_sh...  22.4 us
    unnamed x4, local copies, waits for them, and re-layouts  2.54 us

profile of v2, /device:TPU:0, one launch (start us, length us, event | category | flops | bytes accessed | tf_op | source)
XLA Modules:
  0.0 25.6 jit_solution(5857351001624555878)
XLA Ops:
  0.6 22.4 %hartree.1 = (f32[2,32]{1,0:T(2,128)}, f32[2,16,49]{2,1,0:T(8,128)}) custom-call(s32[3,7680]{1,0:T(4,128)} %miller_hbm.1, bf16[49,7680]{1,0:T(8,128)(2,1)} %form_hbm.1, f32[3,64]{1,0:T(4,128)} %frac_hbm.1, bf16[49,2,64]{2,1,0:T(2,128)(2,1)} %bitcast.2, s32[32]{0:T(128)} %owner_hbm.1, f32[3,32]{1,0:T(4,128)} %offs_hbm.1), custom_call_target="tpu_custom_call" | custom-call | tf_op jit(solution)/shard_map/hartree/pallas_call | solution.py:357
  23.1 0.0 copy-start
  23.1 0.7 %copy-done = f32[2,32]{1,0:T(2,128)S(1)} copy-done((f32[2,32]{1,0:T(2,128)S(1)}, f32[2,32]{1,0:T(2,128)}, u32[]{:S(2)}) %copy-start) | copy-done | bytes 280
  23.7 0.6 %copy.10 = f32[2,32]{1,0:T(2,128)} copy(f32[2,32]{1,0:T(2,128)S(1)} %copy-done) | data formatting | bytes 512
  24.3 1.3 %copy.11 = f32[2,49,16]{1,2,0:T(8,128)} copy(f32[2,49,16]{1,2,0:T(8,128)} %bitcast.3) | data formatting | bytes 12544
Async XLA Ops:
  23.1 0.7 %copy-start = (f32[2,32]{1,0:T(2,128)S(1)}, f32[2,32]{1,0:T(2,128)}, u32[]{:S(2)}) copy-start(f32[2,32]{1,0:T(2,128)} %get-tuple-element.8) | copy-start | bytes 772

commit v3 on v2

--- a/solution.py
+++ b/solution.py
@@ -215,7 +215,7 @@
         arriving.wait()
         summed = partial[core, quarter] + from_core[quarter]
         acc[quarter] = summed
-        chip_out[quarter] = summed.astype(bf16)
+        chip_out[quarter] = summed
         copies = []
         for away in range(1, chips):
             copy = pltpu.make_async_remote_copy(
@@ -234,7 +234,7 @@
         summed = acc[quarter]
         for away, copy in enumerate(copies, 1):
             copy.wait()
-            summed = summed + chip_in[away, quarter].astype(f32)
+            summed = summed + chip_in[away, quarter]
         total[core, quarter] = summed
         copy = pltpu.make_async_remote_copy(
             src_ref=total.at[core, quarter],
@@ -357,8 +357,8 @@
     grid, moments = pl.pallas_call(
         functools.partial(kernel, n_atoms, n_split, chunk),
         out_shape=(
-            jax.ShapeDtypeStruct((dens, own_points), f32),
-            jax.ShapeDtypeStruct((dens, share, comps), f32),
+            pltpu.VMEM((dens, own_points), f32),
+            pltpu.VMEM((dens, share, comps), f32),
         ),
         in_specs=[hbm] * 6,
         out_specs=(vmem, vmem),
@@ -376,8 +376,8 @@
             pltpu.VMEM((2, 2, 2 * dens, width), f32),
             pltpu.VMEM((2, 2 * dens, width), f32),
             pltpu.VMEM((2, 2 * dens, width), f32),
-            pltpu.VMEM((2, 2 * dens, width), bf16),
-            pltpu.VMEM((chips, 2, 2 * dens, width), bf16),
+            pltpu.VMEM((2, 2 * dens, width), f32),
+            pltpu.VMEM((chips, 2, 2 * dens, width), f32),
             pltpu.VMEM((2, 2, 2 * dens, width), f32),
             pltpu.VMEM((n_split, 8, 128), f32),
             pltpu.VMEM((n_split, share + 8, 128), f32),
@@ -395,7 +395,7 @@
             dma((n_split,)),
         ],
         compiler_params=pltpu.CompilerParams(
-            collective_id=0, has_side_effects=True, vmem_limit_bytes=67_043_328
+            collective_id=0, has_side_effects=True, vmem_limit_bytes=60_000_000
         ),
         name="hartree",
     )(

time: 25.9 us -> 24.1 us (0.931)
  local copies, waits for them, and re-layouts: 2.54 us -> 1.17 us
  Pallas kernels: 22.4 us -> 22.1 us
    unnamed x4 -> x2, local copies, waits for them, and re-layouts: 2.54 us -> 1.17 us
    pallas_call x1, Pallas kernels: 22.4 us -> 22.1 us  [shards(): pl.pallas_call(functools.partial(kernel, n_atoms, n_split, chunk), out_sh...]
where the time goes in v3:
time: 24.1 us; the launch traced here: 23.9 us
  Pallas kernels  22.1 us (92%)
  local copies, waits for them, and re-layouts  1.17 us (5%)
  between operations  0.64 us (3%)
    pallas_call x1, Pallas kernels, shards(): pl.pallas_call(functools.partial(kernel, n_atoms, n_split, chunk), out_sh...  22.1 us
    unnamed x2, local copies, waits for them, and re-layouts  1.17 us

profile of v3, /device:TPU:0, one launch (start us, length us, event | category | flops | bytes accessed | tf_op | source)
XLA Modules:
  0.0 23.9 jit_solution(10509762745562002469)
XLA Ops:
  0.6 22.1 %hartree.1 = (f32[2,32]{1,0:T(2,128)S(1)}, f32[2,16,49]{2,1,0:T(8,128)S(1)}) custom-call(s32[3,7680]{1,0:T(4,128)} %miller_hbm.1, bf16[49,7680]{1,0:T(8,128)(2,1)} %form_hbm.1, f32[3,64]{1,0:T(4,128)} %frac_hbm.1, bf16[49,2,64]{2,1,0:T(2,128)(2,1)} %bitcast.3, s32[32]{0:T(128)} %owner_hbm.1, f32[3,32]{1,0:T(4,128)} %offs_hbm.1), custom_call_target="tpu_custom_call" | custom-call | tf_op jit(solution)/shard_map/hartree/pallas_call | solution.py:357
  22.8 0.6 %copy.10 = f32[2,32]{1,0:T(2,128)} copy(f32[2,32]{1,0:T(2,128)S(1)} %get-tuple-element.6) | data formatting | bytes 512
  23.3 0.6 %copy.11 = f32[2,49,16]{1,2,0:T(8,128)} copy(f32[2,49,16]{1,2,0:T(8,128)S(1)} %bitcast.2) | data formatting | bytes 12544
